TPU v7x, 32 devices: a whole 2x2x4 slice. The times are simulated.
32 devices in a mesh: seq: 8 (over z, y), feat: 4 (over x, core).
Axes of the slice: x: 2, y: 2, z: 4, core: 2. Of those that a mesh axis runs over, the one named last changes fastest.
Arguments:
- hidden_in: bfloat16 [4, 2048, 2048], P(None, 'seq'), may hold values from -6 to 6
- w_query: bfloat16 [2048, 256], replicated, may hold values from -0.125 to 0.125
- w_key: bfloat16 [2048, 256], replicated, may hold values from -0.125 to 0.125
- w_value: bfloat16 [2048, 2048], P(None, 'feat'), may hold values from -0.125 to 0.125
- lengths: int32 [4], replicated, may hold values from 1024 to 2048, as said below
- owners: int32 [4], replicated, may hold values from 0 to 7
Outputs:
- mixed: bfloat16 [4, 2048, 2048], P(None, 'seq', 'feat')
- state_quad: float32 [8, 4, 16, 256, 128], P('seq', None, None, 'feat')
- state_low: float32 [8, 4, 16, 17, 128], P('seq', None, 'feat')
- norm_quad: float32 [8, 4, 16, 256], P('seq', None, None, 'feat')
- norm_low: float32 [8, 4, 16, 17], P('seq', None, 'feat')
Inputs may be any that keep to these rules, and one draw needn't show every extreme that they name: `lengths`: every prompt holds 1024 to 2048 live tokens, and some prompt holds exactly 2048. `owners`: several prompts may share a decoding device.
All inputs are finite; a program needn't handle non-finite values.
Results may differ from a plain program's by a relative error of at most 0.0085.
Values may be sent and summed in bfloat16 or wider, within the bound.
A program may use at most 256 MiB of HBM per device.

v0:
```python
import jax
import jax.numpy as jnp
from jax import lax
from jax.sharding import PartitionSpec as P

H = 16
FD = 16
NORM_FLOOR = 0.0001


def prefix(part, axis, combine, identity):
    place = lax.axis_index(axis)
    gathered = jax.tree.map(lambda a: lax.all_gather(a, axis), part)
    state = jax.tree.map(lambda a, e: jnp.zeros_like(a) + jnp.asarray(e, a.dtype), part, identity)

    def one(step, state):
        return combine(
            state, jax.tree.map(lambda a: lax.dynamic_index_in_dim(a, step, 0, False), gathered)
        )

    return lax.fori_loop(0, place, one, state)


def low_features(inputs):
    constant = jnp.ones(inputs.shape[:-1] + (1,), jnp.float32)
    return jnp.concatenate([constant, inputs * FD ** (-0.25)], axis=-1)


def quad_features(leading, inputs):
    products = leading[..., :, None] * inputs[..., None, :]
    return products.reshape(inputs.shape[:-1] + (leading.shape[-1] * inputs.shape[-1],)) * (
        2.0 * FD
    ) ** (-0.5)


def add_states(earlier_part, later_part):
    return jax.tree.map(
        lambda first_term, second_term: first_term + second_term, earlier_part, later_part
    )


def project(flat_rows, weight_cols, prompts, span, heads, width_last):
    projected = jnp.dot(flat_rows, weight_cols, preferred_element_type=jnp.float32).astype(
        jnp.bfloat16
    )
    return projected.reshape(prompts, span, heads, width_last).astype(jnp.float32)


def body(hidden_in, w_query, w_key, w_value, lengths, owners):
    highest = lax.Precision.HIGHEST
    prompts, span, width = hidden_in.shape
    n_feat = lax.axis_size("feat")
    feat_index = lax.axis_index("feat")
    seq_index = lax.axis_index("seq")
    own_heads = H // n_feat
    head_dim = width // H
    flat_rows = hidden_in.reshape(prompts * span, width)
    positions = seq_index * span + jnp.arange(span, dtype=jnp.int32)
    live_mask = (positions[None, :] < lengths[:, None]).astype(jnp.float32)
    key_mask = live_mask[:, :, None, None]
    values_own = jnp.dot(flat_rows, w_value, preferred_element_type=jnp.float32).astype(
        jnp.bfloat16
    )
    value_own = values_own.reshape(prompts, span, own_heads, head_dim).astype(jnp.float32)
    query_cols = lax.dynamic_slice_in_dim(w_query, feat_index * own_heads * FD, own_heads * FD, 1)
    key_cols = lax.dynamic_slice_in_dim(w_key, feat_index * own_heads * FD, own_heads * FD, 1)
    query_own = project(flat_rows, query_cols, prompts, span, own_heads, FD)
    key_own = project(flat_rows, key_cols, prompts, span, own_heads, FD)
    key_quad = quad_features(key_own, key_own) * key_mask
    query_quad = quad_features(query_own, query_own)
    span_quad = jnp.einsum("pchf,pchd->phfd", key_quad, value_own, precision=highest)
    norm_span = jnp.sum(key_quad, axis=1)
    key_low = low_features(key_own) * key_mask
    query_low = low_features(query_own)
    span_low = jnp.einsum("pchf,pchd->phfd", key_low, value_own, precision=highest)
    low_norm = jnp.sum(key_low, axis=1)
    empty_states = (
        jnp.zeros_like(span_quad),
        jnp.zeros_like(norm_span),
        jnp.zeros_like(span_low),
        jnp.zeros_like(low_norm),
    )
    pre_quad, pre_norm, pre_low, pre_lnorm = prefix(
        (span_quad, norm_span, span_low, low_norm), "seq", add_states, empty_states
    )
    final_quad, final_norm, final_low, final_lnorm = lax.psum(
        (span_quad, norm_span, span_low, low_norm), "seq"
    )
    num_low = jnp.einsum("pchf,phfd->pchd", query_low, pre_low, precision=highest)
    den_low = jnp.einsum("pchf,phf->pch", query_low, pre_lnorm, precision=highest)
    num_quad = jnp.einsum("pchf,phfd->pchd", query_quad, pre_quad, precision=highest)
    den_quad = jnp.einsum("pchf,phf->pch", query_quad, pre_norm, precision=highest)
    final_quad, final_norm = (
        lax.all_to_all(final_quad, "feat", split_axis=2, concat_axis=1, tiled=True),
        lax.all_to_all(final_norm, "feat", split_axis=2, concat_axis=1, tiled=True),
    )
    scores = jnp.einsum("pthf,puhf->phtu", query_own, key_own, precision=highest)
    kernel = 1.0 + scores * FD ** (-0.5) + scores * scores * (0.5 / FD)
    causal = (jnp.arange(span)[:, None] >= jnp.arange(span)[None, :]).astype(jnp.float32)
    weight = kernel * causal[None, None, :, :] * live_mask[:, None, None, :]
    num_self = jnp.einsum("phtu,puhd->pthd", weight, value_own, precision=highest)
    den_self = jnp.transpose(jnp.sum(weight, axis=3), (0, 2, 1))
    numerator = num_low + num_quad + num_self
    denominator = den_low + den_quad + den_self
    attended = numerator / denominator[..., None] * live_mask[:, :, None, None]
    squares = jnp.sum(attended * attended, axis=(2, 3))
    sum_squares = lax.psum(squares, "feat")
    scaled = attended * lax.rsqrt(sum_squares / width + NORM_FLOOR)[:, :, None, None]
    mixed = scaled.astype(jnp.bfloat16).reshape(prompts, span, own_heads * head_dim)
    owned = (owners == seq_index).astype(jnp.float32)
    state_quad = (owned[:, None, None, None] * final_quad)[None]
    state_low = (owned[:, None, None, None] * final_low)[None]
    norm_quad = (owned[:, None, None] * final_norm)[None]
    norm_low = (owned[:, None, None] * final_lnorm)[None]
    return (mixed, state_quad, state_low, norm_quad, norm_low)


def solution(mesh):
    placed = (P(None, "seq", None), P(), P(), P(None, "feat"), P(), P())
    return jax.shard_map(
        body,
        mesh=mesh,
        in_specs=placed,
        out_specs=(
            P(None, "seq", "feat"),
            P("seq", None, None, "feat", None),
            P("seq", None, "feat", None, None),
            P("seq", None, None, "feat"),
            P("seq", None, "feat", None),
        ),
        check_vma=False,
    )
```

profile of v0, /device:TPU:0, one launch (start us, length us, event | category | flops | bytes accessed | tf_op | source)
XLA Modules:
  0.0 468.9 jit_solution(4810927062687896524)
XLA Ops:
  7.2 4.2 fusion.9
  12.4 2.8 bitcast_multiply_fusion
  15.2 0.9 copy-done.2
  16.1 3.3 convolution_convert_fusion
  19.3 1.3 reshape.151
  21.3 5.5 %fusion.36 = f32[4,4,256,128]{3,2,1,0:T(8,128)} fusion(f32[4,256,4,256]{1,3,2,0:T(8,128)} %bitcast_multiply_fusion, bf16[4,256,4,128]{1,3,2,0:T(8,128)(2,1)S(1)} %copy.62), kind=kOutput, calls=%fused_computation.68 | convolution fusion | flops 1610612736 | bytes 7340032 | tf_op jit(solution)/shard_map/pchf,pchd->phfd/dot_general | solution.py:71
  27.5 57.1 %all-reduce.2 = (f32[4,4,256]{1,0,2:T(4,128)S(1)}, f32[4,4,17]{2,1,0:T(4,128)S(1)}) all-reduce(f32[4,4,256]{1,0,2:T(4,128)S(1)} %bitcast.91, f32[4,4,17]{2,1,0:T(4,128)S(1)} %fusion.17), channel_id=1, replica_groups=mesh['seq'=8,'feat'=4] {'seq'}, use_global_device_ids=true, to_apply=%region_9.10 | all-reduce | flops 4368 | bytes 34944 | tf_op jit(solution)/shard_map/psum | solution.py:86
  84.7 1.2 reshape.161
  85.8 3.3 all-to-all-start.1
  89.3 0.9 fusion.18
  90.2 0.7 copy.55
  91.1 4.1 fusion.10
  96.1 2.6 multiply_multiply_fusion.1
  98.7 1.5 fusion.1
  100.2 3.9 fusion.2
  104.1 32.0 %all_gather.27 = f32[8,4,4,256]{3,2,1,0:T(4,128)S(1)} all-gather(f32[1,4,4,256]{3,2,1,0:T(4,128)S(1)} %all_gather.26), channel_id=1, replica_groups=mesh['seq'=8,'feat'=4] {'seq'}, dimensions={0}, use_global_device_ids=true | all-gather | bytes 147456 | tf_op jit(solution)/shard_map/all_gather | solution.py:13
  136.1 33.0 %all-gather.2 = f32[32,4,17]{2,1,0:T(4,128)S(1)} all-gather(f32[4,4,17]{2,1,0:T(4,128)S(1)} %fusion.17), channel_id=4, replica_groups=mesh['seq'=8,'feat'=4] {'seq'}, dimensions={0}, use_global_device_ids=true | all-gather | bytes 9792 | tf_op jit(solution)/shard_map/all_gather | solution.py:13
  171.2 0.7 broadcast_multiply_fusion.4
  171.9 94.8 %all-gather.6.cloned.1.call-done = f32[32,4,256,128]{3,2,1,0:T(8,128)} async-done(((f32[4,4,256,128]{3,2,1,0:T(8,128)}), f32[32,4,256,128]{3,2,1,0:T(8,128)}) %all-gather.6.cloned.1.call-update) | async-done | bytes 16777232 | tf_op jit(solution)/shard_map/all_gather | solution.py:13
  266.7 0.7 all-reduce.6.cloned.1.call-update
  267.4 41.0 %all-gather.8.cloned.1.call-done = f32[32,4,17,128]{3,1,2,0:T(4,128)} async-done(((f32[4,4,17,128]{3,1,2,0:T(4,128)}), f32[32,4,17,128]{3,1,2,0:T(4,128)}) %all-gather.8.cloned.1.call-update) | async-done | bytes 1114128 | tf_op jit(solution)/shard_map/all_gather | solution.py:13
  309.3 3.2 fusion.15
  312.4 4.3 fusion.26
  316.7 101.8 %all-reduce.6.cloned.1.call-done = (f32[4,4,256,128]{3,2,1,0:T(8,128)}, f32[4,4,17,128]{3,2,1,0:T(8,128)}) async-done(((f32[4,4,256,128]{3,2,1,0:T(8,128)}, f32[4,4,17,128]{3,2,1,0:T(8,128)}), (f32[4,4,256,128]{3,2,1,0:T(8,128)}, f32[4,4,17,128]{3,2,1,0:T(8,128)})) %all-reduce.6.cloned.1.call-update) | async-done | bytes 2236432 | tf_op jit(solution)/shard_map/psum | solution.py:86
  418.5 4.3 copy.64
  422.8 4.4 all-to-all-start
  427.3 8.3 %multiply_reduce_fusion.1 = (f32[4,256]{1,0:T(4,128)S(1)}, f32[4,256,4,128]{1,3,2,0:T(8,128)}) fusion(f32[4,256]{1,0:T(4,128)S(1)} %compare_convert_fusion, f32[4,256,4]{1,2,0:T(4,128)S(1)} %fusion.25, f32[4,4,128,256]{3,2,1,0:T(8,128)} %fusion.2, f32[4,4,128,256]{3,2,1,0:T(8,128)} %fusion.15, f32[4,4,256,128]{3,2,1,0:T(8,128)S(1)} %get-tuple-element.62, ...), kind=kOutput, calls=%fused_computation.15 | convolution fusion | flops 1613757440 | bytes 12607488 | tf_op jit(solution)/shard_map/pchf,phfd->pchd/dot_general | solution.py:91
  435.6 18.8 %psum.35 = f32[4,256]{1,0:T(4,128)S(1)} all-reduce(f32[4,256]{1,0:T(4,128)S(1)} %get-tuple-element.123), channel_id=1, replica_groups=mesh['seq'=8,'feat'=4] {'feat'}, use_global_device_ids=true, to_apply=%region_6.7 | all-reduce | flops 1024 | bytes 8192 | tf_op jit(solution)/shard_map/psum | solution.py:107
  454.4 1.8 multiply_convert_fusion
  456.3 1.3 copy.69
  458.4 2.4 copy.65
  460.8 1.6 broadcast_multiply_fusion.1
  (51 shorter events, 7.1 us)
Async XLA Ops:
  7.2 8.0 %copy-start = (bf16[2048,512]{1,0:T(8,128)(2,1)S(1)}, bf16[2048,512]{1,0:T(8,128)(2,1)}, u32[]{:S(2)}) copy-start(bf16[2048,512]{1,0:T(8,128)(2,1)} %param.11) | copy-start | bytes 6291460
  7.2 4.4 copy-start.5
  7.2 259.5 %all-gather.6.cloned.1.call-start = ((), (), s32[]{:S(2)}) async-start(), calls=%async_computation.2 | async-start | bytes 18874368 | tf_op jit(solution)/shard_map/all_gather | solution.py:13
  12.4 3.7 copy-start.2
  84.6 10.7 %copy-start.6 = (s32[4]{0:T(128)S(1)}, s32[4]{0:T(128)}, u32[]{:S(2)}) copy-start(s32[4]{0:T(128)} %param.13) | copy-start | bytes 52
  85.8 83.2 %all-to-all-start.1 = ((f32[4,1,1024]{2,1,0:T(1,128)}), f32[4,1,1024]{2,1,0:T(1,128)S(1)}, u32[]{:S(2)}, u32[]{:S(2)}) async-start(f32[4,1,1024]{2,1,0:T(1,128)} %reshape.161), calls=%async_computation.1 | async-start | bytes 32768 | tf_op jit(solution)/shard_map/all_to_all | solution.py:95
  89.1 219.3 %all-gather.8.cloned.1.call-start = ((), (), s32[]{:S(2)}) async-start(), calls=%async_computation.3 | async-start | bytes 1253376 | tf_op jit(solution)/shard_map/all_gather | solution.py:13
  90.2 8.4 %copy-start.3 = (f32[4,4,17,128]{3,2,1,0:T(8,128)}, f32[4,4,17,128]{3,2,1,0:T(8,128)S(1)}, u32[]{:S(2)}) copy-start(f32[4,4,17,128]{3,2,1,0:T(8,128)S(1)} %fusion.18) | copy-start | bytes 417796
  266.6 151.9 %all-reduce.6.cloned.1.call-start = ((), (), s32[]{:S(2)}) async-start(), calls=%async_computation.4 | async-start | bytes 4587520 | tf_op jit(solution)/shard_map/psum | solution.py:86
  422.8 35.6 %all-to-all-start = ((f32[4,4,256,128]{3,1,0,2:T(4,128)}), f32[4,4,256,128]{3,1,0,2:T(4,128)}, u32[]{:S(2)}, u32[]{:S(2)}) async-start(f32[4,4,256,128]{3,1,0,2:T(4,128)} %copy.64), calls=%async_computation | async-start | bytes 4194304 | tf_op jit(solution)/shard_map/all_to_all | solution.py:94
  435.6 22.0 %copy-start.4 = (f32[4,4,17,128]{3,2,1,0:T(8,128)S(1)}, f32[4,4,17,128]{3,2,1,0:T(8,128)}, u32[]{:S(2)}) copy-start(f32[4,4,17,128]{3,2,1,0:T(8,128)} %get-tuple-element.118) | copy-start | bytes 417796
  458.4 4.0 copy-start.1
Sparse Core Ops, SparseCore 0:
  26.9 239.6 all-gather.5
  269.4 38.9 all-gather.7
  312.7 105.7 all-reduce.5
where the time goes:
time: 470 us; the launch traced here: 469 us
  waiting for transfers between devices  238 us (51%)
  blocking collectives  141 us (30%)
  matrix products  39.6 us (8%)
  local copies, waits for them, and re-layouts  15.8 us (3%)
  between operations  14 us (3%)
  other arithmetic  12 us (3%)
  starting transfers between devices  7.96 us (2%)
    all_gather x2, waiting for transfers between devices, prefix(): gathered = jax.tree.map(lambda a: lax.all_gather(a, axis), part)  136 us
    psum x1, waiting for transfers between devices, body(): lax.psum((span_quad, norm_span, span_low, low_norm), 'seq')  102 us
    all_gather x2, blocking collectives, prefix(): gathered = jax.tree.map(lambda a: lax.all_gather(a, axis), part)  65 us
    psum x1, blocking collectives, body(): lax.psum((span_quad, norm_span, span_low, low_norm), 'seq')  57.1 us
    psum x1, blocking collectives, body(): sum_squares = lax.psum(squares, 'feat')  18.8 us
  transfers between devices with their start and end apart: 5, of which 3 were waited for; matrix products, arithmetic and copies ran while one was open for 8% of the time, Pallas kernels for 0%

commit v1 on v0

--- a/solution.py
+++ b/solution.py
@@ -104,7 +104,8 @@
     denominator = den_low + den_quad + den_self
     attended = numerator / denominator[..., None] * live_mask[:, :, None, None]
     squares = jnp.sum(attended * attended, axis=(2, 3))
-    sum_squares = lax.psum(squares, "feat")
+    parts = lax.all_gather(squares, "feat", axis=0, tiled=False)
+    sum_squares = parts.sum(axis=0)
     scaled = attended * lax.rsqrt(sum_squares / width + NORM_FLOOR)[:, :, None, None]
     mixed = scaled.astype(jnp.bfloat16).reshape(prompts, span, own_heads * head_dim)
     owned = (owners == seq_index).astype(jnp.float32)

time: 470 us -> 469 us (level)
    psum x1 -> x0, blocking collectives: 18.8 us -> none  [body(): sum_squares = lax.psum(squares, 'feat')]
    all_gather x0 -> x1, blocking collectives: none -> 18.3 us  [body(): parts = lax.all_gather(squares, 'feat', axis=0, tiled=False)]
where the time goes in v1:
time: 469 us; the launch traced here: 468 us
  waiting for transfers between devices  238 us (51%)
  blocking collectives  140 us (30%)
  matrix products  39.6 us (8%)
  local copies, waits for them, and re-layouts  15.8 us (3%)
  between operations  14 us (3%)
  other arithmetic  12 us (3%)
  starting transfers between devices  7.96 us (2%)
    all_gather x2, waiting for transfers between devices, prefix(): gathered = jax.tree.map(lambda a: lax.all_gather(a, axis), part)  136 us
    psum x1, waiting for transfers between devices, body(): lax.psum((span_quad, norm_span, span_low, low_norm), 'seq')  102 us
    all_gather x2, blocking collectives, prefix(): gathered = jax.tree.map(lambda a: lax.all_gather(a, axis), part)  65 us
    psum x1, blocking collectives, body(): lax.psum((span_quad, norm_span, span_low, low_norm), 'seq')  57.1 us
    all_gather x1, blocking collectives, body(): parts = lax.all_gather(squares, 'feat', axis=0, tiled=False)  18.3 us
  transfers between devices with their start and end apart: 5, of which 3 were waited for; matrix products, arithmetic and copies ran while one was open for 8% of the time, Pallas kernels for 0%

profile of v1, /device:TPU:0, one launch (start us, length us, event | category | flops | bytes accessed | tf_op | source)
XLA Modules:
  0.0 468.4 jit_solution(9084697610891866758)
XLA Ops:
  7.2 4.2 fusion.9
  12.4 2.8 bitcast_multiply_fusion
  15.2 0.9 copy-done.2
  16.1 3.3 convolution_convert_fusion
  19.3 1.3 reshape.155
  21.3 5.5 %fusion.36 = f32[4,4,256,128]{3,2,1,0:T(8,128)} fusion(f32[4,256,4,256]{1,3,2,0:T(8,128)} %bitcast_multiply_fusion, bf16[4,256,4,128]{1,3,2,0:T(8,128)(2,1)S(1)} %copy.62), kind=kOutput, calls=%fused_computation.68 | convolution fusion | flops 1610612736 | bytes 7340032 | tf_op jit(solution)/shard_map/pchf,pchd->phfd/dot_general | solution.py:71
  27.5 57.1 %all-reduce.2 = (f32[4,4,256]{1,0,2:T(4,128)S(1)}, f32[4,4,17]{2,1,0:T(4,128)S(1)}) all-reduce(f32[4,4,256]{1,0,2:T(4,128)S(1)} %bitcast.92, f32[4,4,17]{2,1,0:T(4,128)S(1)} %fusion.17), channel_id=1, replica_groups=mesh['seq'=8,'feat'=4] {'seq'}, use_global_device_ids=true, to_apply=%region_9.10 | all-reduce | flops 4368 | bytes 34944 | tf_op jit(solution)/shard_map/psum | solution.py:86
  84.7 1.2 reshape.169
  85.8 3.3 all-to-all-start.1
  89.3 0.9 fusion.18
  90.2 0.7 copy.55
  91.1 4.1 fusion.10
  96.1 2.6 multiply_multiply_fusion.1
  98.7 1.5 fusion.1
  100.2 3.9 fusion.2
  104.1 32.0 %all_gather.33 = f32[8,4,4,256]{3,2,1,0:T(4,128)S(1)} all-gather(f32[1,4,4,256]{3,2,1,0:T(4,128)S(1)} %all_gather.32), channel_id=1, replica_groups=mesh['seq'=8,'feat'=4] {'seq'}, dimensions={0}, use_global_device_ids=true | all-gather | bytes 147456 | tf_op jit(solution)/shard_map/all_gather | solution.py:13
  136.1 33.0 %all-gather.2 = f32[32,4,17]{2,1,0:T(4,128)S(1)} all-gather(f32[4,4,17]{2,1,0:T(4,128)S(1)} %fusion.17), channel_id=4, replica_groups=mesh['seq'=8,'feat'=4] {'seq'}, dimensions={0}, use_global_device_ids=true | all-gather | bytes 9792 | tf_op jit(solution)/shard_map/all_gather | solution.py:13
  171.2 0.7 broadcast_multiply_fusion.4
  171.9 94.8 %all-gather.8.cloned.1.call-done = f32[32,4,256,128]{3,2,1,0:T(8,128)} async-done(((f32[4,4,256,128]{3,2,1,0:T(8,128)}), f32[32,4,256,128]{3,2,1,0:T(8,128)}) %all-gather.8.cloned.1.call-update) | async-done | bytes 16777232 | tf_op jit(solution)/shard_map/all_gather | solution.py:13
  266.7 0.7 all-reduce.6.cloned.1.call-update
  267.4 41.0 %all-gather.10.cloned.1.call-done = f32[32,4,17,128]{3,1,2,0:T(4,128)} async-done(((f32[4,4,17,128]{3,1,2,0:T(4,128)}), f32[32,4,17,128]{3,1,2,0:T(4,128)}) %all-gather.10.cloned.1.call-update) | async-done | bytes 1114128 | tf_op jit(solution)/shard_map/all_gather | solution.py:13
  309.3 3.2 fusion.15
  312.4 4.3 fusion.26
  316.7 101.8 %all-reduce.6.cloned.1.call-done = (f32[4,4,256,128]{3,2,1,0:T(8,128)}, f32[4,4,17,128]{3,2,1,0:T(8,128)}) async-done(((f32[4,4,256,128]{3,2,1,0:T(8,128)}, f32[4,4,17,128]{3,2,1,0:T(8,128)}), (f32[4,4,256,128]{3,2,1,0:T(8,128)}, f32[4,4,17,128]{3,2,1,0:T(8,128)})) %all-reduce.6.cloned.1.call-update) | async-done | bytes 2236432 | tf_op jit(solution)/shard_map/psum | solution.py:86
  418.5 4.3 copy.64
  422.8 4.4 all-to-all-start
  427.3 8.3 %multiply_reduce_fusion.1 = (f32[4,256]{1,0:T(4,128)S(1)}, f32[4,256,4,128]{1,3,2,0:T(8,128)}) fusion(f32[4,256]{1,0:T(4,128)S(1)} %compare_convert_fusion, f32[4,256,4]{1,2,0:T(4,128)S(1)} %fusion.25, f32[4,4,128,256]{3,2,1,0:T(8,128)} %fusion.2, f32[4,4,128,256]{3,2,1,0:T(8,128)} %fusion.15, f32[4,4,256,128]{3,2,1,0:T(8,128)S(1)} %get-tuple-element.62, ...), kind=kOutput, calls=%fused_computation.15 | convolution fusion | flops 1613757440 | bytes 12607488 | tf_op jit(solution)/shard_map/pchf,phfd->pchd/dot_general | solution.py:91
  435.6 18.3 %all-gather.4 = f32[4,4,256]{2,1,0:T(4,128)S(1)} all-gather(f32[1,4,256]{2,1,0:T(4,128)S(1)} %bitcast.100), channel_id=5, replica_groups=mesh['seq'=8,'feat'=4] {'feat'}, dimensions={0}, use_global_device_ids=true | all-gather | bytes 20480 | tf_op jit(solution)/shard_map/all_gather | solution.py:107
  453.9 1.8 multiply_convert_fusion
  455.7 1.3 copy.69
  457.8 2.4 copy.65
  460.3 1.6 broadcast_multiply_fusion.1
  (52 shorter events, 7.1 us)
Async XLA Ops:
  7.2 8.0 %copy-start = (bf16[2048,512]{1,0:T(8,128)(2,1)S(1)}, bf16[2048,512]{1,0:T(8,128)(2,1)}, u32[]{:S(2)}) copy-start(bf16[2048,512]{1,0:T(8,128)(2,1)} %param.11) | copy-start | bytes 6291460
  7.2 4.4 copy-start.5
  7.2 259.5 %all-gather.8.cloned.1.call-start = ((), (), s32[]{:S(2)}) async-start(), calls=%async_computation.2 | async-start | bytes 18874368 | tf_op jit(solution)/shard_map/all_gather | solution.py:13
  12.4 3.7 copy-start.2
  84.6 10.7 %copy-start.6 = (s32[4]{0:T(128)S(1)}, s32[4]{0:T(128)}, u32[]{:S(2)}) copy-start(s32[4]{0:T(128)} %param.13) | copy-start | bytes 52
  85.8 83.2 %all-to-all-start.1 = ((f32[4,1,1024]{2,1,0:T(1,128)}), f32[4,1,1024]{2,1,0:T(1,128)S(1)}, u32[]{:S(2)}, u32[]{:S(2)}) async-start(f32[4,1,1024]{2,1,0:T(1,128)} %reshape.169), calls=%async_computation.1 | async-start | bytes 32768 | tf_op jit(solution)/shard_map/all_to_all | solution.py:95
  89.1 219.3 %all-gather.10.cloned.1.call-start = ((), (), s32[]{:S(2)}) async-start(), calls=%async_computation.3 | async-start | bytes 1253376 | tf_op jit(solution)/shard_map/all_gather | solution.py:13
  90.2 8.4 %copy-start.3 = (f32[4,4,17,128]{3,2,1,0:T(8,128)}, f32[4,4,17,128]{3,2,1,0:T(8,128)S(1)}, u32[]{:S(2)}) copy-start(f32[4,4,17,128]{3,2,1,0:T(8,128)S(1)} %fusion.18) | copy-start | bytes 417796
  266.6 151.9 %all-reduce.6.cloned.1.call-start = ((), (), s32[]{:S(2)}) async-start(), calls=%async_computation.4 | async-start | bytes 4587520 | tf_op jit(solution)/shard_map/psum | solution.py:86
  422.8 35.1 %all-to-all-start = ((f32[4,4,256,128]{3,1,0,2:T(4,128)}), f32[4,4,256,128]{3,1,0,2:T(4,128)}, u32[]{:S(2)}, u32[]{:S(2)}) async-start(f32[4,4,256,128]{3,1,0,2:T(4,128)} %copy.64), calls=%async_computation | async-start | bytes 4194304 | tf_op jit(solution)/shard_map/all_to_all | solution.py:94
  435.6 21.4 %copy-start.4 = (f32[4,4,17,128]{3,2,1,0:T(8,128)S(1)}, f32[4,4,17,128]{3,2,1,0:T(8,128)}, u32[]{:S(2)}) copy-start(f32[4,4,17,128]{3,2,1,0:T(8,128)} %get-tuple-element.118) | copy-start | bytes 417796
  457.8 4.0 copy-start.1
Sparse Core Ops, SparseCore 0:
  26.9 239.6 all-gather.7
  269.4 38.9 all-gather.9
  312.7 105.7 all-reduce.5
